TPU v7x, 32 devices: a whole 2x2x4 slice. The times are simulated.
32 devices in a mesh: walk: 4 (over y, x), orb: 8 (over z, core).
Axes of the slice: x: 2, y: 2, z: 4, core: 2. Of those that a mesh axis runs over, the one named last changes fastest.
Arguments:
- coefficients: bfloat16 [4096, 4096], P(None, 'orb'), may hold values from -6 to 6
- inverse: bfloat16 [4, 1024, 1024], P('walk', 'orb'), may hold values from -0.005859375 to 0.005859375
- cell_index: int32 [4, 3, 1024], P('walk'), may hold values from 0 to 15
- fraction: float32 [4, 3, 1024], P('walk'), may hold values from 0 to 1
- energies: float32 [4], P('walk'), may hold values from -8 to 8
- weights: float32 [4], P('walk'), may hold values from 0.5 to 2
- occupied: int32 [1024], replicated, may hold values from 0 to 4095, as said below
Outputs:
- gradient: float32 [1024, 4096], P('walk', 'orb')
Inputs may be any that keep to these rules, and one draw needn't show every extreme that they name: `occupied`: 1024 distinct orbital indices; every block of 512 consecutive orbital indices holds at most 192 of them, and some block holds exactly 192.
All inputs are finite; a program needn't handle non-finite values.
Results may differ from a plain program's by a relative error of at most 0.019.
Values may be sent and summed in bfloat16 or wider, within the bound.
A program may use at most 64 MiB of HBM per device.

v0:
```python
import jax
import jax.numpy as jnp
from jax import lax
from jax.sharding import PartitionSpec as P

GRID = 16


def spline_basis(frac):
    remain = 1.0 - frac
    square = frac * frac
    cubed = square * frac
    values = (
        jnp.stack(
            [
                remain * remain * remain,
                3.0 * cubed - 6.0 * square + 4.0,
                -3.0 * cubed + 3.0 * square + 3.0 * frac + 1.0,
                cubed,
            ]
        )
        / 6.0
    )
    curves = jnp.stack([remain, 3.0 * frac - 2.0, 1.0 - 3.0 * frac, frac])
    return (values, curves)


def evaluate(coefficients, cell_one, frac_one, edge):
    shifts = jnp.arange(4, dtype=jnp.int32)[:, None] - 1
    index_x = (cell_one[0][None, :] + shifts) % edge
    index_y = (cell_one[1][None, :] + shifts) % edge
    index_z = (cell_one[2][None, :] + shifts) % edge
    value_x, curve_x = spline_basis(frac_one[0])
    value_y, curve_y = spline_basis(frac_one[1])
    value_z, curve_z = spline_basis(frac_one[2])
    plane = (index_y[:, None, :] * edge + index_z[None, :, :]).reshape(16, -1)
    value_yz = (value_y[:, None, :] * value_z[None, :, :]).reshape(16, -1)
    curve_yz = (
        curve_y[:, None, :] * value_z[None, :, :] + value_y[:, None, :] * curve_z[None, :, :]
    ).reshape(16, -1)
    electrons = cell_one.shape[1]
    orb_width = coefficients.shape[1]
    all_rows = (index_x[:, None, :] * (edge * edge) + plane[None, :, :]).reshape(64, electrons)
    weight_val = (value_x[:, None, :] * value_yz[None, :, :]).reshape(64, electrons)
    weight_lap = (
        curve_x[:, None, :] * value_yz[None, :, :] + value_x[:, None, :] * curve_yz[None, :, :]
    ).reshape(64, electrons)
    val_high = weight_val.astype(jnp.bfloat16)
    val_low = (weight_val - val_high.astype(jnp.float32)).astype(jnp.bfloat16)
    lap_high = weight_lap.astype(jnp.bfloat16)
    lap_low = (weight_lap - lap_high.astype(jnp.float32)).astype(jnp.bfloat16)
    stacked = jnp.stack([val_high, val_low, lap_high, lap_low])
    block = 256
    count = electrons // block
    rows_blocked = jnp.transpose(all_rows.reshape(64, count, block), (1, 2, 0))
    weights_blocked = jnp.transpose(stacked.reshape(4, 64, count, block), (2, 3, 0, 1))

    def one_block(items):
        rows_one, weights_one = items
        gathered = jnp.take(coefficients, rows_one, axis=0)
        parts = jnp.einsum(
            "nqk,nkw->nqw", weights_one, gathered, preferred_element_type=jnp.float32
        )
        orbital_sum = parts[:, 0, :] + parts[:, 1, :]
        laplace_sum = parts[:, 2, :] + parts[:, 3, :]
        return jnp.concatenate(
            [orbital_sum.astype(jnp.bfloat16), laplace_sum.astype(jnp.bfloat16)], axis=1
        )

    results = lax.map(one_block, (rows_blocked, weights_blocked))
    return results.reshape(electrons, 2 * orb_width)


def apply_inverse(inverse_rows, both_vals):
    return jnp.dot(
        lax.all_gather(inverse_rows, "orb", axis=0, tiled=True),
        both_vals,
        preferred_element_type=jnp.float32,
    )


def slot_tables(occupied, shard_index, orb_width, capacity):
    mine = occupied // orb_width == shard_index
    ranking = jnp.cumsum(mine.astype(jnp.int32)) - 1
    slot_ids = jnp.arange(capacity, dtype=jnp.int32)
    placed = mine[None, :] & (ranking[None, :] == slot_ids[:, None])
    positions = jnp.arange(occupied.shape[0], dtype=jnp.int32)
    slot_rows = jnp.sum(jnp.where(placed, positions[None, :], 0), axis=1)
    local_cols = occupied - shard_index * orb_width
    slot_cols = jnp.sum(jnp.where(placed, local_cols[None, :], 0), axis=1)
    filled = jnp.any(placed, axis=1)
    picker = (
        (jnp.arange(orb_width, dtype=jnp.int32)[:, None] == slot_cols[None, :]) & filled[None, :]
    ).astype(jnp.bfloat16)
    return (picker, slot_rows)


def couple_slots(kinetic_low, ratio, picker, slot_rows):
    slot_block = jnp.einsum(
        "ls,nl->sn", picker, kinetic_low, preferred_element_type=jnp.float32
    ).astype(jnp.bfloat16)
    ratio_rows = jnp.take(ratio, lax.all_gather(slot_rows, "orb", axis=0, tiled=True), axis=0)
    return jnp.einsum(
        "sn,sw->nw",
        lax.all_gather(slot_block, "orb", axis=0, tiled=True),
        ratio_rows,
        preferred_element_type=jnp.float32,
    )


def body(coefficients, inverse, cell_index, fraction, energies, weights, occupied):
    orb_width = coefficients.shape[1]
    orb_count = lax.axis_size("orb")
    shard_index = lax.axis_index("orb")
    electrons = occupied.shape[0]
    capacity = 3 * electrons // (2 * orb_count)
    picker, slot_rows = slot_tables(occupied, shard_index, orb_width, capacity)
    running = jnp.zeros((electrons, orb_width), jnp.float32)

    def finish(running, products, energy, weight):
        ratio = products[:, :orb_width].astype(jnp.bfloat16)
        kinetic = products[:, orb_width:]
        kinetic_low = kinetic.astype(jnp.bfloat16)
        coupled = couple_slots(kinetic_low, ratio, picker, slot_rows)
        sample_term = weight * (energy * ratio.astype(jnp.float32) - 0.5 * (kinetic - coupled))
        return running + sample_term

    def step_each(running, items):
        inverse_one, cells_one, frac_one, energy, weight = items
        products = apply_inverse(inverse_one, evaluate(coefficients, cells_one, frac_one, GRID))
        return (finish(running, products, energy, weight), None)

    running, unused = lax.scan(
        step_each, running, (inverse, cell_index, fraction, energies, weights)
    )
    return lax.psum_scatter(
        running.astype(jnp.bfloat16), "walk", scatter_dimension=0, tiled=True
    ).astype(jnp.float32)


def solution(mesh):
    in_specs = (
        P(None, "orb"),
        P("walk", "orb", None),
        P("walk", None, None),
        P("walk", None, None),
        P("walk"),
        P("walk"),
        P(),
    )
    out_specs = P("walk", "orb")
    return jax.shard_map(body, mesh=mesh, in_specs=in_specs, out_specs=out_specs, check_vma=False)
```

profile of v0, /device:TPU:1, one launch (start us, length us, event | category | flops | bytes accessed | tf_op | source)
XLA Modules:
  0.0 425.3 jit_solution(14278239120757062725)
XLA Ops:
  6.5 0.7 all-gather.6.cloned.1.call-update
  7.3 0.8 fusion.27
  8.1 0.8 broadcast_subtract_fusion.3
  10.4 324.0 %while.17 = (s32[]{:T(128)}, bf16[4,256,1024]{2,1,0:T(8,128)(2,1)}, bf16[4,256,4,64]{1,0,3,2:T(4,128)(2,1)S(1)}, s32[4,256,64]{1,0,2:T(4,128)S(1)}, bf16[4096,512]{1,0:T(8,128)(2,1)}, /*index=5*/s32[]{:T(128)}) while((s32[]{:T(128)}, bf16[4,256,1024]{2,1,0:T(8,128)(2,1)}, bf16[4,256,4,64]{1,0,3,2:T(4,128)(2,1)S(1)}, ...), condition=%wide.region_1.2_spmd, body=%wide.region_0.1_spmd.sunk | while | flops 77234176 | bytes 58622540 | solution.py:70
  10.8 69.3 %gather_fusion = bf16[16384,512]{1,0:T(8,128)(2,1)} fusion(bf16[4096,512]{1,0:T(8,128)(2,1)} %get-tuple-element.195, s32[16384]{0:T(1024)S(1)} %broadcast_clamp_fusion.2), kind=kCustom, calls=%fused_computation.clone.1 | custom fusion | bytes 33619968 | tf_op jit(solution)/shard_map/while/body/eval_jaxpr/while/body/eval_jaxpr/jit(_take)/gather | solution.py:60
  80.6 8.4 %fusion.48 = f32[256,4,512]{2,1,0:T(4,128)S(1)} fusion(bf16[256,64,512]{2,1,0:T(8,128)(2,1)} %bitcast.94, pred[256,64]{1,0:T(8,128)(4,1)S(1)} %compare_and_fusion.3, bf16[1,256,4,64]{3,2,1,0:T(4,128)(2,1)S(1)} %copy.40), kind=kOutput, calls=%fused_computation.2.clone.1 | convolution fusion | flops 75497472 | bytes 19021824 | tf_op jit(solution)/shard_map/while/body/eval_jaxpr/while/body/eval_jaxpr/nqk,nkw->nqw/dot_general | solution.py:61
  89.0 1.4 fusion.49
  90.6 0.9 fusion.50
  91.7 69.3 %gather_fusion = bf16[16384,512]{1,0:T(8,128)(2,1)} fusion(bf16[4096,512]{1,0:T(8,128)(2,1)} %get-tuple-element.195, s32[16384]{0:T(1024)S(1)} %broadcast_clamp_fusion.2), kind=kCustom, calls=%fused_computation.clone.1 | custom fusion | bytes 33619968 | tf_op jit(solution)/shard_map/while/body/eval_jaxpr/while/body/eval_jaxpr/jit(_take)/gather | solution.py:60
  161.6 8.4 %fusion.48 = f32[256,4,512]{2,1,0:T(4,128)S(1)} fusion(bf16[256,64,512]{2,1,0:T(8,128)(2,1)} %bitcast.94, pred[256,64]{1,0:T(8,128)(4,1)S(1)} %compare_and_fusion.3, bf16[1,256,4,64]{3,2,1,0:T(4,128)(2,1)S(1)} %copy.40), kind=kOutput, calls=%fused_computation.2.clone.1 | convolution fusion | flops 75497472 | bytes 19021824 | tf_op jit(solution)/shard_map/while/body/eval_jaxpr/while/body/eval_jaxpr/nqk,nkw->nqw/dot_general | solution.py:61
  170.0 1.4 fusion.49
  171.6 0.9 fusion.50
  172.7 69.3 %gather_fusion = bf16[16384,512]{1,0:T(8,128)(2,1)} fusion(bf16[4096,512]{1,0:T(8,128)(2,1)} %get-tuple-element.195, s32[16384]{0:T(1024)S(1)} %broadcast_clamp_fusion.2), kind=kCustom, calls=%fused_computation.clone.1 | custom fusion | bytes 33619968 | tf_op jit(solution)/shard_map/while/body/eval_jaxpr/while/body/eval_jaxpr/jit(_take)/gather | solution.py:60
  242.6 8.4 %fusion.48 = f32[256,4,512]{2,1,0:T(4,128)S(1)} fusion(bf16[256,64,512]{2,1,0:T(8,128)(2,1)} %bitcast.94, pred[256,64]{1,0:T(8,128)(4,1)S(1)} %compare_and_fusion.3, bf16[1,256,4,64]{3,2,1,0:T(4,128)(2,1)S(1)} %copy.40), kind=kOutput, calls=%fused_computation.2.clone.1 | convolution fusion | flops 75497472 | bytes 19021824 | tf_op jit(solution)/shard_map/while/body/eval_jaxpr/while/body/eval_jaxpr/nqk,nkw->nqw/dot_general | solution.py:61
  251.0 1.4 fusion.49
  252.6 0.9 fusion.50
  253.7 69.3 %gather_fusion = bf16[16384,512]{1,0:T(8,128)(2,1)} fusion(bf16[4096,512]{1,0:T(8,128)(2,1)} %get-tuple-element.195, s32[16384]{0:T(1024)S(1)} %broadcast_clamp_fusion.2), kind=kCustom, calls=%fused_computation.clone.1 | custom fusion | bytes 33619968 | tf_op jit(solution)/shard_map/while/body/eval_jaxpr/while/body/eval_jaxpr/jit(_take)/gather | solution.py:60
  323.6 8.4 %fusion.48 = f32[256,4,512]{2,1,0:T(4,128)S(1)} fusion(bf16[256,64,512]{2,1,0:T(8,128)(2,1)} %bitcast.94, pred[256,64]{1,0:T(8,128)(4,1)S(1)} %compare_and_fusion.3, bf16[1,256,4,64]{3,2,1,0:T(4,128)(2,1)S(1)} %copy.40), kind=kOutput, calls=%fused_computation.2.clone.1 | convolution fusion | flops 75497472 | bytes 19021824 | tf_op jit(solution)/shard_map/while/body/eval_jaxpr/while/body/eval_jaxpr/nqk,nkw->nqw/dot_general | solution.py:61
  332.0 1.4 fusion.49
  333.5 0.9 fusion.50
  335.7 4.6 %convolution_bitcast_fusion = f32[1024,1024]{0,1:T(8,128)S(1)} fusion(bf16[1024,1024]{1,0:T(8,128)(2,1)} %bitcast.27, bf16[1,1024,1024]{2,1,0:T(8,128)(2,1)} %all-gather.6.cloned.1.call-done), kind=kOutput, calls=%fused_computation.22 | convolution fusion | flops 2147483648 | bytes 8388608 | tf_op jit(solution)/shard_map/while/body/eval_jaxpr/dot_general | solution.py:75
  340.3 1.9 copy-done
  342.2 1.2 convolution_convert_fusion
  344.7 0.6 dynamic-slice
  346.3 8.7 %all-reduce = s32[1536]{0:T(1024)S(1)} all-reduce(s32[1536]{0:T(1024)S(1)} %dynamic-update-slice), channel_id=1, replica_groups=mesh['walk'=4,'orb'=8] {'orb'}, use_global_device_ids=true, to_apply=%add | all-reduce | flops 1536 | bytes 12288
  355.0 1.7 slice.116
  356.8 0.5 copy.25
  357.3 4.8 %gather_fusion.1 = bf16[1536,512]{1,0:T(8,128)(2,1)S(1)} fusion(bf16[1024,512]{1,0:T(8,128)(2,1)S(1)} %copy.25, s32[2048]{0:T(1024)S(1)} %pad_clamp_fusion), kind=kCustom, calls=%fused_computation.1 | custom fusion | bytes 3151872 | tf_op jit(solution)/shard_map/while/body/eval_jaxpr/jit(_take)/gather | solution.py:102
  362.2 22.1 %all-gather.4.cloned.1.call-done = bf16[1536,1024]{1,0:T(8,128)(2,1)} async-done(((bf16[192,1024]{1,0:T(8,128)(2,1)}), bf16[1536,1024]{1,0:T(8,128)(2,1)}) %all-gather.4.cloned.1.call-update) | async-done | bytes 3145744 | tf_op jit(solution)/shard_map/while/body/eval_jaxpr/all_gather | solution.py:105
  384.3 6.2 %multiply_convert_fusion = bf16[1024,512]{0,1:T(8,128)(2,1)} fusion(f32[1024,1024]{0,1:T(8,128)} %copy-done, bf16[1536,1024]{1,0:T(8,128)(2,1)} %all-gather.4.cloned.1.call-done, bf16[1536,512]{1,0:T(8,128)(2,1)S(1)} %gather_fusion.1, pred[1536]{0:T(1024)(128)(4,1)S(1)} %compare_and_fusion.1, f32[]{:T(128)} %bitcast.92, f32[]{:T(128)} %bitcast.93), kind=kOutput, calls=%fused_computation.25 | convolution fusion | flops 1615069184 | bytes 8914440 | tf_op jit(solution)/shard_map/while/body/eval_jaxpr/sn,sw->nw/dot_general | solution.py:103
  390.5 26.4 %reduce-scatter.2.cloned.1.call-done = bf16[256,512]{0,1:T(8,128)(2,1)} async-done(((bf16[1024,512]{0,1:T(8,128)(2,1)}), bf16[256,512]{0,1:T(8,128)(2,1)}) %reduce-scatter.2.cloned.1.call-update) | async-done | bytes 262160 | tf_op jit(solution)/shard_map/reduce_scatter | solution.py:136
  416.9 1.9 copy.27
  (83 shorter events, 6.8 us)
Async XLA Ops:
  6.5 3.1 copy-start.2
  6.5 329.1 %all-gather.6.cloned.1.call-start = ((), (), s32[]{:S(2)}) async-start(), calls=%async_computation.3 | async-start | bytes 2359296 | tf_op jit(solution)/shard_map/while/body/eval_jaxpr/all_gather | solution.py:76
  7.3 377.0 %all-gather.4.cloned.1.call-start = ((), (), s32[]{:S(2)}) async-start(), calls=%async_computation.1 | async-start | bytes 3538944 | tf_op jit(solution)/shard_map/while/body/eval_jaxpr/all_gather | solution.py:105
  10.4 324.0 %copy-start.1 = (s32[1024]{0:T(1024)S(1)}, s32[1024]{0:T(1024)}, u32[]{:S(2)}) copy-start(s32[1024]{0:T(1024)} %param.15) | copy-start | bytes 12292
  340.3 1.9 copy-start
  340.3 4.5 %copy-start.3 = (u32[32]{0:T(128)S(1)}, u32[32]{0:T(128)}, u32[]{:S(2)}) copy-start(u32[32]{0:T(128)} %constant.156) | copy-start | bytes 388
  343.4 73.5 %reduce-scatter.2.cloned.1.call-start = ((), (), s32[]{:S(2)}) async-start(), calls=%async_computation.2 | async-start | bytes 1310720 | tf_op jit(solution)/shard_map/reduce_scatter | solution.py:136
Sparse Core Ops, SparseCore 0:
  8.9 31.5 all-gather.5
  343.5 40.6 all-gather.3
  390.6 26.2 reduce-scatter.1
where the time goes:
time: 427 us; the launch traced here: 425 us
  local copies, waits for them, and re-layouts  293 us (69%)
  waiting for transfers between devices  49.3 us (12%)
  matrix products  45.6 us (11%)
  between operations  15.3 us (4%)
  other arithmetic  12.9 us (3%)
  blocking collectives  8.72 us (2%)
    gather x4, local copies, waits for them, and re-layouts, one_block(): gathered = jnp.take(coefficients, rows_one, axis=0)  277 us
    dot_general x4, matrix products, one_block(): jnp.einsum('nqk,nkw->nqw', weights_one, gathered, preferred_element_type=...  33.7 us
    reduce_scatter x1, waiting for transfers between devices, body(): lax.psum_scatter(running.astype(jnp.bfloat16), 'walk', scatter_dimension=...  26.4 us
    all_gather x1, waiting for transfers between devices, couple_slots(): lax.all_gather(slot_block, 'orb', axis=0, tiled=True)  22.1 us
    unnamed x1, blocking collectives  8.72 us
  transfers between devices with their start and end apart: 3, of which 2 were waited for; matrix products, arithmetic and copies ran while one was open for 79% of the time, Pallas kernels for 0%

commit v1 on v0

v1 whole, which is shorter than its diff:
```python
import functools
import jax
import jax.numpy as jnp
from jax import lax
from jax.experimental import pallas as pl
from jax.experimental.pallas import tpu as pltpu
from jax.sharding import PartitionSpec as P

GRID = 16
PLANE = GRID * GRID
MESH = pl.DeviceIdType.MESH
F32 = jnp.float32
BF16 = jnp.bfloat16
CONTRACT_LANES = (((1,), (1,)), ((), ()))


def spline_rows(frac):
    remain = 1.0 - frac
    square = frac * frac
    cubed = square * frac
    sixth = 1.0 / 6.0
    values = [
        remain * remain * remain * sixth,
        (3.0 * cubed - 6.0 * square + 4.0) * sixth,
        (-3.0 * cubed + 3.0 * square + 3.0 * frac + 1.0) * sixth,
        cubed * sixth,
    ]
    curves = [remain, 3.0 * frac - 2.0, 1.0 - 3.0 * frac, frac]
    return values, curves


def dense_tables(cell, frac):
    electrons = cell.shape[1]
    line = lax.broadcasted_iota(jnp.int32, (GRID, electrons), 0)
    values, curves = spline_rows(frac)
    value = jnp.zeros((GRID, electrons), F32)
    curve = jnp.zeros((GRID, electrons), F32)
    for tap in range(4):
        hit = line == ((cell + (GRID + tap - 1)) & (GRID - 1))
        value = value + jnp.where(hit, values[tap], 0.0)
        curve = curve + jnp.where(hit, curves[tap], 0.0)
    return value, curve


class LineGather:
    def __init__(self, buf, rows, chips, z, core, sems):
        self.buf, self.rows, self.chips, self.z, self.core = buf, rows, chips, z, core
        self.send, self.recv, self.sib_send, self.sib_recv = sems

    def block(self, owner):
        return self.buf.at[pl.ds(pl.multiple_of(owner * self.rows, self.rows), self.rows), :]

    def copy(self, owner, send, recv, target):
        return pltpu.make_async_remote_copy(
            src_ref=self.block(owner),
            dst_ref=self.block(owner),
            send_sem=send,
            recv_sem=recv,
            device_id={"orb": target},
            device_id_type=MESH,
        )

    def hop(self, way, k):
        sign = 1 - 2 * way
        chip = self.z - sign * k
        onto = self.z + sign
        copy = self.copy(
            chip * 2 + self.core, self.send.at[way, k], self.recv.at[way, k], onto * 2 + self.core
        )
        return copy, (chip >= 0) & (chip < self.chips) & (onto >= 0) & (onto < self.chips)

    def came(self, way, k):
        sign = 1 - 2 * way
        chip = self.z - sign * (k + 1)
        copy = self.copy(
            chip * 2 + self.core, self.send.at[way, k], self.recv.at[way, k], self.z * 2 + 1 - self.core
        )
        return chip, copy, (chip >= 0) & (chip < self.chips)

    def relay(self, chip, owner_core, slot):
        return self.copy(
            chip * 2 + owner_core, self.sib_send.at[slot], self.sib_recv.at[slot],
            self.z * 2 + 1 - self.core,
        )

    def step(self, k):
        if k == 0:
            for way in range(2):
                copy, sends = self.hop(way, 0)
                pl.when(sends)(copy.start)
            self.relay(self.z, self.core, 0).start()
            return
        for way in range(2):
            chip, arrived, comes = self.came(way, k - 1)
            pl.when(comes)(arrived.wait_recv)
            if k < self.chips - 1:
                copy, sends = self.hop(way, k)
                pl.when(sends)(copy.start)
            pl.when(comes)(self.relay(chip, self.core, 1 + 2 * (k - 1) + way).start)

    def sibling(self, k):
        if k == 0:
            self.relay(self.z, 1 - self.core, 0).wait_recv()
            return
        for way in range(2):
            chip, _, comes = self.came(way, k - 1)
            pl.when(comes)(self.relay(chip, 1 - self.core, 1 + 2 * (k - 1) + way).wait_recv)

    def drain(self):
        self.relay(self.z, self.core, 0).wait_send()
        for k in range(self.chips - 1):
            for way in range(2):
                copy, sends = self.hop(way, k)
                pl.when(sends)(copy.wait_send)
                chip, _, comes = self.came(way, k)
                pl.when(comes)(self.relay(chip, self.core, 1 + 2 * k + way).wait_send)


def kernel(
    dims,
    coef_hbm, inv_ref, cell_ref, frac_ref, energy_ref, weight_ref, occ_ref,
    out_ref,
    coef, inv_all, sel_all, xt, yzv, yzl, w_scr, phi, lap, ratio, rsel, total, send_buf, recv_buf,
    coef_sem, own_sem, i_send, i_recv, i_sib_send, i_sib_recv,
    s_send, s_recv, s_sib_send, s_sib_recv, g_send, g_recv,
):
    walkers, orbs, capacity, block = dims
    chips = orbs // 2
    electrons = cell_ref.shape[2]
    width = coef.shape[1]
    inv_rows = inv_ref.shape[1]
    out_rows = out_ref.shape[0]
    me_walk = lax.axis_index("walk")
    me_orb = lax.axis_index("orb")
    z = me_orb // 2
    core = me_orb % 2

    load = pltpu.make_async_copy(coef_hbm, coef, coef_sem)
    load.start()
    gather_inv = LineGather(inv_all, inv_rows, chips, z, core, (i_send, i_recv, i_sib_send, i_sib_recv))
    gather_sel = LineGather(sel_all, capacity, chips, z, core, (s_send, s_recv, s_sib_send, s_sib_recv))
    own = pltpu.make_async_copy(inv_ref.at[0], gather_inv.block(me_orb), own_sem)
    own.start()

    barrier = pltpu.get_barrier_semaphore()
    pl.semaphore_signal(barrier, inc=1, device_id={"orb": z * 2 + 1 - core}, device_id_type=MESH)
    for step in range(1, walkers):
        peer = lax.rem(me_walk + step, walkers)
        pl.semaphore_signal(barrier, inc=1, device_id={"walk": peer}, device_id_type=MESH)

    @pl.when(z > 0)
    def _():
        pl.semaphore_signal(barrier, inc=1, device_id={"orb": me_orb - 2}, device_id_type=MESH)

    @pl.when(z < chips - 1)
    def _():
        pl.semaphore_signal(barrier, inc=1, device_id={"orb": me_orb + 2}, device_id_type=MESH)

    neighbours = jnp.where(z > 0, 1, 0) + jnp.where(z < chips - 1, 1, 0)
    pl.semaphore_wait(barrier, walkers + neighbours)

    own.wait()
    gather_inv.step(0)

    xv, xc = dense_tables(cell_ref[0, 0:1, :], frac_ref[0, 0:1, :])
    yv, yc = dense_tables(cell_ref[0, 1:2, :], frac_ref[0, 1:2, :])
    zv, zc = dense_tables(cell_ref[0, 2:3, :], frac_ref[0, 2:3, :])
    xt[0:GRID, :] = xv
    xt[GRID:2 * GRID, :] = xc
    xt[2 * GRID:, :] = jnp.zeros((xt.shape[0] - 2 * GRID, electrons), F32)
    for y in range(GRID):
        at = slice(y * GRID, (y + 1) * GRID)
        yzv[at, :] = yv[y:y + 1, :] * zv
        yzl[at, :] = yc[y:y + 1, :] * zv + yv[y:y + 1, :] * zc

    occ = occ_ref[...]
    owner = occ // width
    ones = lax.broadcasted_iota(jnp.int32, (orbs, electrons), 0) == owner
    before = (
        lax.broadcasted_iota(jnp.int32, (electrons, electrons), 0)
        < lax.broadcasted_iota(jnp.int32, (electrons, electrons), 1)
    )
    counts = jnp.dot(
        jnp.where(ones, 1.0, 0.0).astype(BF16), jnp.where(before, 1.0, 0.0).astype(BF16),
        preferred_element_type=F32,
    )
    rank = jnp.sum(jnp.where(ones, counts, 0.0), axis=0, keepdims=True)
    slot = owner * capacity + rank.astype(jnp.int32)
    local = occ - me_orb * width
    row_hit = lax.broadcasted_iota(jnp.int32, (width, electrons), 0) == local
    my_slot = slot - me_orb * capacity
    slot_hit = (lax.broadcasted_iota(jnp.int32, (capacity, electrons), 0) == my_slot)
    picker = lax.dot_general(
        jnp.where(slot_hit, 1.0, 0.0).astype(BF16), jnp.where(row_hit, 1.0, 0.0).astype(BF16),
        CONTRACT_LANES, preferred_element_type=F32,
    ).astype(BF16)

    load.wait()

    def evaluate(at, carry):
        cols = pl.ds(pl.multiple_of(at * block, block), block)
        x_tab = jnp.transpose(xt[:, cols])
        plane_v = jnp.transpose(yzv[:, cols])
        plane_l = jnp.transpose(yzl[:, cols])
        for x in range(GRID):
            val = x_tab[:, x:x + 1]
            cur = x_tab[:, GRID + x:GRID + x + 1]
            lanes = slice(x * PLANE, (x + 1) * PLANE)
            w_scr[0:block, lanes] = (val * plane_v).astype(BF16)
            w_scr[block:, lanes] = (cur * plane_v + val * plane_l).astype(BF16)
        both = jnp.dot(w_scr[...], coef[...], preferred_element_type=F32)
        phi[:, cols] = jnp.transpose(both[0:block]).astype(BF16)
        lap[:, cols] = jnp.transpose(both[block:]).astype(BF16)
        return carry

    trips = electrons // block
    lax.fori_loop(0, trips // 2, evaluate, 0)
    gather_inv.step(1)
    lax.fori_loop(trips // 2, trips, evaluate, 0)
    mine = pl.ds(pl.multiple_of(me_orb * capacity, capacity), capacity)
    sel_all[mine, :] = jnp.dot(picker, lap[...], preferred_element_type=F32).astype(BF16)
    gather_sel.step(0)
    for k in range(2, chips):
        gather_inv.step(k)
    for k in range(chips):
        gather_inv.sibling(k)
    if chips > 1:
        pass

    def ratio_block(chip, carry):
        rows = pl.ds(pl.multiple_of(chip * 2 * inv_rows, 2 * inv_rows), 2 * inv_rows)
        ratio[:, rows] = lax.dot_general(
            phi[...], inv_all[rows, :], CONTRACT_LANES, preferred_element_type=F32
        ).astype(BF16)
        return carry

    lax.fori_loop(0, chips, ratio_block, 0)

    pair = 2 * capacity

    def pick_block(chip, carry):
        hit = lax.broadcasted_iota(jnp.int32, (pair, electrons), 0) + chip * pair == slot
        rsel[pl.ds(chip, 1)] = lax.dot_general(
            ratio[...], jnp.where(hit, 1.0, 0.0).astype(BF16), CONTRACT_LANES,
            preferred_element_type=F32,
        ).astype(BF16)[None]
        return carry

    lax.fori_loop(0, chips, pick_block, 0)

    energy = energy_ref[0]
    weight = weight_ref[0]
    total[...] = (weight * energy) * phi[...].astype(F32) - (0.5 * weight) * lap[...].astype(F32)

    def couple(chip):
        rows = pl.ds(pl.multiple_of(chip * pair, pair), pair)
        total[...] += (0.5 * weight) * jnp.dot(
            rsel[pl.ds(chip, 1)][0], sel_all[rows, :], preferred_element_type=F32
        )

    gather_sel.sibling(0)
    couple(z)
    for k in range(1, chips):
        gather_sel.step(k)
        gather_sel.sibling(k)
        if k < chips - 1 or chips <= 1:
            pass
        for way in range(2):
            chip, _, comes = gather_sel.came(way, k - 1)
            pl.when(comes)(functools.partial(couple, chip))

    phi[...] = total[...].astype(BF16)

    def product(peer):
        rows = pl.ds(pl.multiple_of(peer * out_rows, out_rows), out_rows)
        return lax.dot_general(
            inv_all[rows, :], phi[...], CONTRACT_LANES, preferred_element_type=F32
        )

    copies = []
    for step in range(1, walkers):
        peer = lax.rem(me_walk + walkers - step, walkers)
        send_buf[step - 1] = product(peer).astype(BF16)
        copy = pltpu.make_async_remote_copy(
            src_ref=send_buf.at[step - 1],
            dst_ref=recv_buf.at[step - 1],
            send_sem=g_send.at[step - 1],
            recv_sem=g_recv.at[step - 1],
            device_id={"walk": peer},
            device_id_type=MESH,
        )
        copy.start()
        copies.append(copy)
    out_ref[...] = product(me_walk)
    for step, copy in enumerate(copies):
        copy.wait_recv()
        out_ref[...] += recv_buf[step].astype(F32)
    for copy in copies:
        copy.wait_send()
    gather_inv.drain()
    gather_sel.drain()


def body(coefficients, inverse, cell_index, fraction, energies, weights, occupied):
    walkers = lax.axis_size("walk")
    orbs = lax.axis_size("orb")
    chips = orbs // 2
    cells, width = coefficients.shape
    inv_rows = inverse.shape[1]
    electrons = inverse.shape[2]
    capacity = 3 * electrons // (2 * orbs)
    block = min(256, electrons)
    out_rows = electrons // walkers
    dims = (walkers, orbs, capacity, block)
    dma = pltpu.SemaphoreType.DMA
    hops = (2, max(chips - 1, 1))
    relays = (1 + 2 * (chips - 1),)
    vmem = pl.BlockSpec(memory_space=pltpu.VMEM)
    smem = pl.BlockSpec(memory_space=pltpu.SMEM)
    return pl.pallas_call(
        functools.partial(kernel, dims),
        out_shape=jax.ShapeDtypeStruct((out_rows, width), F32),
        in_specs=[pl.BlockSpec(memory_space=pl.ANY), vmem, vmem, vmem, smem, smem, vmem],
        out_specs=vmem,
        scratch_shapes=[
            pltpu.VMEM((cells, width), BF16),
            pltpu.VMEM((electrons, electrons), BF16),
            pltpu.VMEM((orbs * capacity, electrons), BF16),
            pltpu.VMEM((128, electrons), F32),
            pltpu.VMEM((PLANE, electrons), F32),
            pltpu.VMEM((PLANE, electrons), F32),
            pltpu.VMEM((2 * block, cells), BF16),
            pltpu.VMEM((width, electrons), BF16),
            pltpu.VMEM((width, electrons), BF16),
            pltpu.VMEM((width, electrons), BF16),
            pltpu.VMEM((chips, width, 2 * capacity), BF16),
            pltpu.VMEM((width, electrons), F32),
            pltpu.VMEM((max(walkers - 1, 1), out_rows, width), BF16),
            pltpu.VMEM((max(walkers - 1, 1), out_rows, width), BF16),
            dma, dma,
            dma(hops), dma(hops), dma(relays), dma(relays),
            dma(hops), dma(hops), dma(relays), dma(relays),
            dma((max(walkers - 1, 1),)), dma((max(walkers - 1, 1),)),
        ],
        compiler_params=pltpu.CompilerParams(
            collective_id=0, has_side_effects=True, vmem_limit_bytes=60 * 1024 * 1024
        ),
        name="gradient",
    )(coefficients, inverse, cell_index, fraction, energies, weights, occupied.reshape(1, electrons))


def solution(mesh):
    in_specs = (
        P(None, "orb"),
        P("walk", "orb", None),
        P("walk", None, None),
        P("walk", None, None),
        P("walk"),
        P("walk"),
        P(),
    )
    out_specs = P("walk", "orb")
    return jax.shard_map(body, mesh=mesh, in_specs=in_specs, out_specs=out_specs, check_vma=False)
```

time: 427 us -> 73 us (0.17)
  local copies, waits for them, and re-layouts: 293 us -> 4.49 us
  Pallas kernels: 0 us -> 66.9 us
  waiting for transfers between devices: 49.3 us -> 0 us
  matrix products: 45.6 us -> 0 us
  between operations: 15.3 us -> 1.31 us
  other arithmetic: 12.9 us -> 0 us
  blocking collectives: 8.72 us -> 0 us
    gather x5 -> x0, local copies, waits for them, and re-layouts: 282 us -> none  [the longest x4 277 us: one_block(): gathered = jnp.take(coefficients, rows_one, axis=0)]
    pallas_call x0 -> x1, Pallas kernels: none -> 66.9 us  [body(): pl.pallas_call(functools.partial(kernel, dims), out_shape=jax.ShapeDtypeS...]
    dot_general x7 -> x0, matrix products: 45.6 us -> none  [the longest x4 33.7 us: one_block(): jnp.einsum('nqk,nkw->nqw', weights_one, gathered, preferred_element_type=...]
    reduce_scatter x1 -> x0, waiting for transfers between devices: 26.4 us -> none  [body(): lax.psum_scatter(running.astype(jnp.bfloat16), 'walk', scatter_dimension=...]
    all_gather x2 -> x0, waiting for transfers between devices: 22.1 us -> none  [the longest x1 22.1 us: couple_slots(): lax.all_gather(slot_block, 'orb', axis=0, tiled=True)]
    unnamed x1 -> x0, blocking collectives: 8.72 us -> none
    convert_element_type x6 -> x0, other arithmetic: 5.75 us -> none  [the longest x4 5.61 us: one_block(): orbital_sum.astype(jnp.bfloat16)]
  transfers between devices with their start and end apart: 3 -> 0, of which waited for: 2 -> 0; matrix products, arithmetic and copies ran while one was open for 79% -> 0% of each run, Pallas kernels for 0% -> 0%
where the time goes in v1:
time: 73 us; the launch traced here: 72.7 us
  Pallas kernels  66.9 us (92%)
  local copies, waits for them, and re-layouts  4.49 us (6%)
  between operations  1.31 us (2%)
    pallas_call x1, Pallas kernels, body(): pl.pallas_call(functools.partial(kernel, dims), out_shape=jax.ShapeDtypeS...  66.9 us
    unnamed x3, local copies, waits for them, and re-layouts  4.49 us

profile of v1, /device:TPU:1, one launch (start us, length us, event | category | flops | bytes accessed | tf_op | source)
XLA Modules:
  0.0 72.7 jit_solution(2435138596284448266)
XLA Ops:
  1.3 1.3 %copy.8.cell_ref = s32[1,3,1024]{2,1,0:T(4,128)} copy(s32[1,3,1024]{2,0,1:T(1,128)} %param.9) | data formatting | bytes 24576 | tf_op args[2]
  2.6 1.3 %copy.9.frac_ref = f32[1,3,1024]{2,1,0:T(4,128)} copy(f32[1,3,1024]{2,0,1:T(1,128)} %param.10) | data formatting | bytes 24576 | tf_op args[3]
  3.9 66.9 %gradient.1 = f32[256,512]{1,0:T(8,128)} custom-call(bf16[4096,512]{1,0:T(8,128)(2,1)} %coef_hbm.1, bf16[1,128,1024]{2,1,0:T(8,128)(2,1)} %inv_ref.1, s32[1,3,1024]{2,1,0:T(4,128)} %copy.8.cell_ref, f32[1,3,1024]{2,1,0:T(4,128)} %copy.9.frac_ref, f32[1]{0:T(128)S(6)} %copy.11.energy_ref, f32[1]{0:T(128)S(6)} %copy.12.weight_ref, s32[1,1024]{1,0:T(1,128)} %bitcast.1), custom_call_target="tpu_custom_call" | custom-call | tf_op jit(solution)/shard_map/gradient/pallas_call | solution.py:320
  70.9 1.9 %copy.13 = f32[256,512]{1,0:T(8,128)} copy(f32[256,512]{1,0:T(8,128)} %gradient.1) | data formatting | bytes 1048576

commit v2 on v1

--- a/solution.py
+++ b/solution.py
@@ -197,7 +197,12 @@
 
     load.wait()
 
+    trips = electrons // block
+    within = max(1, min(chips, trips - 1))
+
     def evaluate(at, carry):
+        for k in range(1, within):
+            pl.when(at == k + 1)(functools.partial(gather_inv.step, k))
         cols = pl.ds(pl.multiple_of(at * block, block), block)
         x_tab = jnp.transpose(xt[:, cols])
         plane_v = jnp.transpose(yzv[:, cols])
@@ -213,19 +218,14 @@
         lap[:, cols] = jnp.transpose(both[block:]).astype(BF16)
         return carry
 
-    trips = electrons // block
-    lax.fori_loop(0, trips // 2, evaluate, 0)
-    gather_inv.step(1)
-    lax.fori_loop(trips // 2, trips, evaluate, 0)
+    lax.fori_loop(0, trips, evaluate, 0)
     mine = pl.ds(pl.multiple_of(me_orb * capacity, capacity), capacity)
     sel_all[mine, :] = jnp.dot(picker, lap[...], preferred_element_type=F32).astype(BF16)
     gather_sel.step(0)
-    for k in range(2, chips):
+    for k in range(within, chips):
         gather_inv.step(k)
     for k in range(chips):
         gather_inv.sibling(k)
-    if chips > 1:
-        pass
 
     def ratio_block(chip, carry):
         rows = pl.ds(pl.multiple_of(chip * 2 * inv_rows, 2 * inv_rows), 2 * inv_rows)
@@ -235,6 +235,8 @@
         return carry
 
     lax.fori_loop(0, chips, ratio_block, 0)
+    if chips > 1:
+        gather_sel.step(1)
 
     pair = 2 * capacity
 
@@ -261,10 +263,9 @@
     gather_sel.sibling(0)
     couple(z)
     for k in range(1, chips):
-        gather_sel.step(k)
+        if k > 1:
+            gather_sel.step(k)
         gather_sel.sibling(k)
-        if k < chips - 1 or chips <= 1:
-            pass
         for way in range(2):
             chip, _, comes = gather_sel.came(way, k - 1)
             pl.when(comes)(functools.partial(couple, chip))

time: 73 us -> 73.9 us (1.012)
  Pallas kernels: 66.9 us -> 67.8 us
    pallas_call x1, Pallas kernels: 66.9 us -> 67.8 us  [body(): pl.pallas_call(functools.partial(kernel, dims), out_shape=jax.ShapeDtypeS...]
where the time goes in v2:
time: 73.9 us; the launch traced here: 73.6 us
  Pallas kernels  67.8 us (92%)
  local copies, waits for them, and re-layouts  4.49 us (6%)
  between operations  1.31 us (2%)
    pallas_call x1, Pallas kernels, body(): pl.pallas_call(functools.partial(kernel, dims), out_shape=jax.ShapeDtypeS...  67.8 us
    unnamed x3, local copies, waits for them, and re-layouts  4.49 us

profile of v2, /device:TPU:1, one launch (start us, length us, event | category | flops | bytes accessed | tf_op | source)
XLA Modules:
  0.0 73.6 jit_solution(14838568234250591815)
XLA Ops:
  1.3 1.3 %copy.8.cell_ref = s32[1,3,1024]{2,1,0:T(4,128)} copy(s32[1,3,1024]{2,0,1:T(1,128)} %param.9) | data formatting | bytes 24576 | tf_op args[2]
  2.6 1.3 %copy.9.frac_ref = f32[1,3,1024]{2,1,0:T(4,128)} copy(f32[1,3,1024]{2,0,1:T(1,128)} %param.10) | data formatting | bytes 24576 | tf_op args[3]
  3.9 67.8 %gradient.1 = f32[256,512]{1,0:T(8,128)} custom-call(bf16[4096,512]{1,0:T(8,128)(2,1)} %coef_hbm.1, bf16[1,128,1024]{2,1,0:T(8,128)(2,1)} %inv_ref.1, s32[1,3,1024]{2,1,0:T(4,128)} %copy.8.cell_ref, f32[1,3,1024]{2,1,0:T(4,128)} %copy.9.frac_ref, f32[1]{0:T(128)S(6)} %copy.11.energy_ref, f32[1]{0:T(128)S(6)} %copy.12.weight_ref, s32[1,1024]{1,0:T(1,128)} %bitcast.1), custom_call_target="tpu_custom_call" | custom-call | tf_op jit(solution)/shard_map/gradient/pallas_call | solution.py:321
  71.7 1.9 %copy.13 = f32[256,512]{1,0:T(8,128)} copy(f32[256,512]{1,0:T(8,128)} %gradient.1) | data formatting | bytes 1048576
